TPU v7x, 128 devices: a whole 4x4x4 slice. The times are simulated.
128 devices in a mesh: rep: 4 (over y_hi, core), dp: 32 (over y_lo, z, x).
Axes of the slice: x: 4, y: 4 (y_hi: 2, y_lo: 2; y = y_hi * 2 + y_lo), z: 4, core: 2. Of those that a mesh axis runs over, the one named last changes fastest.
Arguments:
- query_states: bfloat16 [1024, 32, 768], P(('rep', 'dp')), may hold values from -12 to 12
- passage_states: bfloat16 [512, 180, 768], P(('rep', 'dp')), may hold values from -12 to 12
- query_lengths: int32 [1024], P(('rep', 'dp')), may hold values from 8 to 32, as said below
- passage_lengths: int32 [512], P(('rep', 'dp')), may hold values from 45 to 180, as said below
- passage_ids: int32 [512, 180], P(('rep', 'dp')), may hold values from 2 to 30521, as said below
- positives: int32 [1024], P(('rep', 'dp')), may hold values from 0 to 127, as said below
- up_weight: bfloat16 [768, 3072], replicated, may hold values from -0.21875 to 0.21875
- up_bias: float32 [3072], replicated, may hold values from -3 to 3
- down_weight: bfloat16 [3072, 768], replicated, may hold values from -0.109375 to 0.109375
- down_bias: float32 [768], replicated, may hold values from -3 to 3
- norm_gain: float32 [768], replicated, may hold values from 0.5 to 1.5
- norm_bias: float32 [768], replicated, may hold values from -2 to 2
- proj_weight: bfloat16 [768, 128], replicated, may hold values from -0.21875 to 0.21875
Outputs:
- mean_loss: float32 [], replicated
- passage_grad: float32 [512, 180, 128], P(('rep', 'dp'))
- proj_grad: float32 [768, 128], replicated
Inputs may be any that keep to these rules, and one draw needn't show every extreme that they name: `query_lengths`: every device holds a query with all 32 slots real. `passage_lengths`: every device holds a passage with all 180 slots real. `passage_ids`: slots 0 and 1 of every passage hold ids 101 and 2; ids 999 to 1066 are punctuation. `positives`: index of the positive passage among the 128 passages of the query's replica group, in the order of the devices.
All inputs are finite; a program needn't handle non-finite values.
Results may differ from a plain program's by a relative error of at most 0.0055.
Values may be sent and summed in bfloat16 or wider, within the bound.
A program may use at most 128 MiB of HBM per device.

v0:
```python
import math
import jax
import jax.numpy as jnp
from jax import lax
from jax.sharding import PartitionSpec as P

temper = 0.05
eps_norm = 1e-06
punct_low = 999
punct_high = 1067


def in_one_piece(arrays, axis, dim, along):
    widths = [math.prod(a.shape[along:]) for a in arrays]
    both = jnp.concatenate(
        [a.reshape(*a.shape[:along], w) for a, w in zip(arrays, widths)], axis=along
    )
    out = lax.all_gather(both, axis, axis=dim, tiled=True)
    blocks = jnp.split(out, [sum(widths[:k]) for k in range(1, len(widths))], axis=along)
    return tuple((b.reshape(*out.shape[:along], *a.shape[along:]) for a, b in zip(arrays, blocks)))


def in_blocks(array, dim, peers):
    before, after = (array.shape[:dim], array.shape[dim + 1 :])
    return jnp.moveaxis(array.reshape(*before, peers, -1, *after), dim, 0)


def summed_on_arrival(array, axis, dim):
    blocks = in_blocks(array, dim, lax.axis_size(axis))
    arrived = lax.all_to_all(blocks, axis, split_axis=0, concat_axis=0, tiled=True)
    return arrived.astype(jnp.float32).sum(axis=0)


def encode_rows(
    token_rows, up_weight, up_bias, down_weight, down_bias, norm_gain, norm_bias, proj_weight
):
    upward = jnp.dot(token_rows, up_weight, preferred_element_type=jnp.float32) + up_bias
    activated = jax.nn.gelu(upward, approximate=False).astype(jnp.bfloat16)
    residual = (
        token_rows.astype(jnp.float32)
        + jnp.dot(activated, down_weight, preferred_element_type=jnp.float32)
        + down_bias
    )
    average = jnp.mean(residual, -1, keepdims=True)
    centered = residual - average
    variance = jnp.mean(centered * centered, -1, keepdims=True)
    hidden = (centered * lax.rsqrt(variance + eps_norm) * norm_gain + norm_bias).astype(
        jnp.bfloat16
    )
    projected = jnp.dot(hidden, proj_weight, preferred_element_type=jnp.float32)
    inverse = lax.rsqrt(jnp.sum(projected * projected, -1, keepdims=True) + eps_norm)
    return (hidden, projected * inverse, inverse)


def token_scores(query_flat, query_keep, block_emb, block_keep, query_count):
    item_count, pass_len, embed_dim = block_emb.shape
    flat_block = block_emb.reshape(item_count * pass_len, embed_dim)
    similar = lax.dot_general(
        query_flat, flat_block, (((1,), (1,)), ((), ())), preferred_element_type=jnp.float32
    )
    weights = (
        jnp.exp(similar / temper).reshape(-1, item_count, pass_len)
        * block_keep.astype(jnp.float32)[None]
    )
    totals = jnp.sum(weights, -1)
    soft_max = temper * jnp.log(totals) * query_keep[:, None]
    scores = jnp.sum(soft_max.reshape(query_count, -1, item_count), 1)
    return (scores, weights, totals)


def token_grads(query_flat, query_keep, block_emb, weights, totals, dscore, query_count):
    item_count, pass_len, embed_dim = block_emb.shape
    factor = (dscore[:, None, :] * query_keep.reshape(query_count, -1)[:, :, None]).reshape(
        -1, item_count
    ) / totals
    sim_grad = (
        (weights * factor[:, :, None]).reshape(-1, item_count * pass_len).astype(jnp.bfloat16)
    )
    flat_block = block_emb.reshape(item_count * pass_len, embed_dim)
    passage_term = lax.dot_general(
        sim_grad, query_flat, (((0,), (0,)), ((), ())), preferred_element_type=jnp.float32
    )
    query_term = jnp.dot(sim_grad, flat_block, preferred_element_type=jnp.float32)
    return (passage_term.reshape(item_count, pass_len, embed_dim), query_term)


def cross_entropy(scores, positives):
    log_total = jnp.log(jnp.sum(jnp.exp(scores), 1))
    onehot = (jnp.arange(scores.shape[1], dtype=jnp.int32)[None, :] == positives[:, None]).astype(
        jnp.float32
    )
    loss_sum = jnp.sum(log_total - jnp.sum(scores * onehot, 1))
    dscore = jnp.exp(scores - log_total[:, None]) - onehot
    return (loss_sum, dscore)


def norm_backward(gradient, normed, inverse):
    return (inverse * (gradient - normed * jnp.sum(normed * gradient, -1, keepdims=True))).astype(
        jnp.bfloat16
    )


def per_device(
    query_states,
    passage_states,
    query_lengths,
    passage_lengths,
    passage_ids,
    positives,
    up_weight,
    up_bias,
    down_weight,
    down_bias,
    norm_gain,
    norm_bias,
    proj_weight,
):
    query_count, query_len, model_width = query_states.shape
    pass_count, pass_len, _ = passage_states.shape
    embed_dim = proj_weight.shape[1]
    token_rows = jnp.concatenate(
        [query_states.reshape(-1, model_width), passage_states.reshape(-1, model_width)], 0
    )
    hidden, normed, inverse = encode_rows(
        token_rows, up_weight, up_bias, down_weight, down_bias, norm_gain, norm_bias, proj_weight
    )
    boundary = query_count * query_len
    query_emb = normed[:boundary].astype(jnp.bfloat16)
    pass_emb = normed[boundary:].astype(jnp.bfloat16).reshape(pass_count, pass_len, embed_dim)
    query_keep = (
        (jnp.arange(query_len, dtype=jnp.int32)[None, :] < query_lengths[:, None])
        .astype(jnp.float32)
        .reshape(-1)
    )
    is_punct = (passage_ids >= punct_low) & (passage_ids < punct_high)
    pass_keep = (
        (jnp.arange(pass_len, dtype=jnp.int32)[None, :] < passage_lengths[:, None])
        & jnp.logical_not(is_punct)
    ).astype(jnp.bfloat16)
    groups = lax.axis_size("dp")
    query_shaped = query_emb.reshape(query_count, query_len, embed_dim)
    keep_shaped = query_keep.astype(jnp.bfloat16).reshape(query_count, query_len)
    gathered, gathered_keep = in_one_piece((query_shaped, keep_shaped), "dp", 0, 2)
    group_query = query_count * groups
    block_query = math.gcd(group_query, 16)
    block_count = group_query // block_query
    query_blocks = gathered.reshape(block_count, block_query * query_len, embed_dim)
    keep_blocks = gathered_keep.astype(jnp.float32).reshape(block_count, block_query * query_len)

    def forward(paired):
        scores, _, _ = token_scores(paired[0], paired[1], pass_emb, pass_keep, block_query)
        return scores

    scores = lax.map(forward, (query_blocks, keep_blocks)).reshape(group_query, pass_count)
    owned_rows = lax.all_to_all(scores, "dp", split_axis=0, concat_axis=1, tiled=True)
    loss_sum, dscore = cross_entropy(owned_rows, positives)
    returned = lax.all_to_all(dscore, "dp", split_axis=1, concat_axis=0, tiled=True)
    grad_blocks = returned.reshape(block_count, block_query, pass_count)

    def backward(pass_grad, triple):
        block_emb, block_keep, block_grad = triple
        _, weights, totals = token_scores(block_emb, block_keep, pass_emb, pass_keep, block_query)
        passage_term, query_term = token_grads(
            block_emb, block_keep, pass_emb, weights, totals, block_grad, block_query
        )
        return (pass_grad + passage_term, query_term)

    start_grad = jnp.zeros((pass_count, pass_len, embed_dim), jnp.float32)
    passage_grad, query_terms = lax.scan(
        backward, start_grad, (query_blocks, keep_blocks, grad_blocks)
    )
    query_grad = summed_on_arrival(
        query_terms.reshape(group_query, query_len, embed_dim).astype(jnp.bfloat16), "dp", 0
    )
    query_grad = query_grad.reshape(query_count * query_len, embed_dim)
    query_back = norm_backward(query_grad, normed[:boundary], inverse[:boundary])
    pass_back = norm_backward(
        passage_grad.reshape(-1, embed_dim), normed[boundary:], inverse[boundary:]
    )
    all_back = jnp.concatenate([query_back, pass_back], 0)
    local_sum = lax.dot_general(
        hidden, all_back, (((0,), (0,)), ((), ())), preferred_element_type=jnp.float32
    )
    proj_total, loss_total = lax.psum((local_sum, loss_sum), ("rep", "dp"))
    mean_loss = loss_total / (query_count * lax.axis_size("rep") * groups)
    return (mean_loss, passage_grad, proj_total)


def solution(mesh):
    in_specs = (
        P(("rep", "dp"), None, None),
        P(("rep", "dp"), None, None),
        P(("rep", "dp")),
        P(("rep", "dp")),
        P(("rep", "dp"), None),
        P(("rep", "dp")),
        P(),
        P(),
        P(),
        P(),
        P(),
        P(),
        P(),
    )
    out_specs = (P(), P(("rep", "dp"), None, None), P())
    return jax.shard_map(
        per_device, mesh=mesh, in_specs=in_specs, out_specs=out_specs, check_vma=False
    )
```

profile of v0, /device:TPU:1, one launch (start us, length us, event | category | flops | bytes accessed | tf_op | source)
XLA Modules:
  0.0 595.7 jit_solution(12372179383174552325)
XLA Ops:
  7.2 1.4 copy.36
  9.8 39.0 %fusion.79 = (f32[976]{0:T(1024)S(1)}, f32[976,768]{1,0:T(8,128)S(1)}) fusion(f32[768]{0:T(1024)} %param.26, bf16[3072,768]{1,0:T(8,128)(2,1)} %param.25, f32[3072]{0:T(1024)} %param.24, bf16[768,3072]{1,0:T(8,128)(2,1)} %param.23, bf16[720,768]{1,0:T(8,128)(2,1)} %reshape.220, bf16[256,768]{1,0:T(8,128)(2,1)} %bitcast.103), kind=kOutput, calls=%fused_computation.118 | convolution fusion | flops 9416821760 | bytes 13953856 | tf_op jit(solution)/shard_map/dot_general | solution.py:41
  53.0 139.8 %all-gather.2.cloned.1.call-done = bf16[256,32,129]{2,1,0:T(8,128)(2,1)} async-done(((bf16[8,32,129]{2,1,0:T(8,128)(2,1)}), bf16[256,32,129]{2,1,0:T(8,128)(2,1)}) %all-gather.2.cloned.1.call-update) | async-done | bytes 2113552 | tf_op jit(solution)/shard_map/all_gather | solution.py:18
  192.8 2.7 convert_reduce_fusion
  195.6 3.3 split.8
  198.9 31.5 %while.23 = (s32[]{:T(128)}, f32[16,16,4]{1,0,2:T(8,128)S(1)}, bf16[16,512,128]{2,1,0:T(8,128)(2,1)}, bf16[720,128]{1,0:T(8,128)(2,1)S(1)}, bf16[4,180]{1,0:T(4,...) while((s32[]{:T(128)}, f32[16,16,4]{1,0,2:T(8,128)S(1)}, bf16[16,512,128]{2,1,0:T(8,128)(2,1)}, ...), condition=%wide.region_6.7_spmd, body=%wide.region_3.6_spmd.sunk | while | flops 95480976 | bytes 6281597 | solution.py:154
  198.9 1.3 multiply_exponential_fusion.4
  200.9 1.3 multiply_exponential_fusion.4
  202.9 1.3 multiply_exponential_fusion.4
  204.8 1.3 multiply_exponential_fusion.4
  206.8 1.3 multiply_exponential_fusion.4
  208.8 1.3 multiply_exponential_fusion.4
  210.8 1.3 multiply_exponential_fusion.4
  212.7 1.3 multiply_exponential_fusion.4
  214.7 1.3 multiply_exponential_fusion.4
  216.7 1.3 multiply_exponential_fusion.4
  218.6 1.3 multiply_exponential_fusion.4
  222.6 1.3 multiply_exponential_fusion.4
  224.5 1.3 multiply_exponential_fusion.4
  228.5 1.3 multiply_exponential_fusion.4
  231.2 6.2 %all-to-all-start = ((f32[32,8,4]{1,2,0:T(4,128)}), f32[32,8,4]{1,2,0:T(4,128)S(1)}, u32[]{:S(2)}, u32[]{:S(2)}) async-start(f32[32,8,4]{1,2,0:T(4,128)} %copy.39), calls=%async_computation | async-start | bytes 131072 | tf_op jit(solution)/shard_map/all_to_all | solution.py:155
  237.4 7.2 %all-to-all-done = f32[32,8,4]{1,2,0:T(4,128)S(1)} async-done(((f32[32,8,4]{1,2,0:T(4,128)}), f32[32,8,4]{1,2,0:T(4,128)S(1)}, u32[]{:S(2)}, u32[]{:S(2)}) %all-to-all-start) | async-done | bytes 4128 | tf_op jit(solution)/shard_map/all_to_all | solution.py:155
  246.1 3.9 all-to-all-start.1
  249.9 7.2 %all-to-all-done.1 = f32[8,32,4]{0,2,1:T(4,128)S(1)} async-done(((f32[8,32,4]{0,2,1:T(4,128)}), f32[8,32,4]{0,2,1:T(4,128)S(1)}, u32[]{:S(2)}, u32[]{:S(2)}) %all-to-all-start.1) | async-done | bytes 4128 | tf_op jit(solution)/shard_map/all_to_all | solution.py:157
  257.2 134.8 %while.24 = (s32[]{:T(128)}, f32[4,180,128]{2,1,0:T(8,128)}, bf16[16,512,128]{2,1,0:T(8,128)(2,1)}, bf16[16,512,128]{2,1,0:T(8,128)(2,1)}, bf16[720,128]{1,0:T(8...) while((s32[]{:T(128)}, f32[4,180,128]{2,1,0:T(8,128)}, ...), condition=%wide.region_13.14_spmd.clone, body=%wide.region_11.13_spmd.clone.sunk | while | flops 285514432 | bytes 21625324 | solution.py:169
  260.6 1.7 multiply_convert_fusion.3
  263.5 1.3 convolution_add_fusion.2
  269.0 1.7 multiply_convert_fusion.3
  271.9 1.3 convolution_add_fusion.2
  277.4 1.7 multiply_convert_fusion.3
  280.3 1.3 convolution_add_fusion.2
  285.8 1.7 multiply_convert_fusion.3
  288.8 1.3 convolution_add_fusion.2
  294.2 1.7 multiply_convert_fusion.3
  297.2 1.3 convolution_add_fusion.2
  302.7 1.7 multiply_convert_fusion.3
  305.6 1.3 convolution_add_fusion.2
  311.1 1.7 multiply_convert_fusion.3
  314.0 1.3 convolution_add_fusion.2
  319.5 1.7 multiply_convert_fusion.3
  322.4 1.3 convolution_add_fusion.2
  327.9 1.7 multiply_convert_fusion.3
  330.9 1.3 convolution_add_fusion.2
  336.4 1.7 multiply_convert_fusion.3
  339.3 1.3 convolution_add_fusion.2
  344.8 1.7 multiply_convert_fusion.3
  347.7 1.3 convolution_add_fusion.2
  353.2 1.7 multiply_convert_fusion.3
  356.1 1.3 convolution_add_fusion.2
  361.6 1.7 multiply_convert_fusion.3
  364.6 1.3 convolution_add_fusion.2
  370.1 1.7 multiply_convert_fusion.3
  373.0 1.3 convolution_add_fusion.2
  378.5 1.7 multiply_convert_fusion.3
  381.4 1.3 convolution_add_fusion.2
  386.9 1.7 multiply_convert_fusion.3
  389.8 1.3 convolution_add_fusion.2
  392.0 4.9 all-to-all-start.2
  398.5 15.8 %all-to-all-done.2 = bf16[32,8,32,128]{3,2,1,0:T(8,128)(2,1)} async-done(((bf16[32,8,32,128]{3,2,1,0:T(8,128)(2,1)}), bf16[32,8,32,128]{3,2,1,0:T(8,128)(2,1)}, u32[]{:S(2)}, u32[]{:S(2)}) %all-to-all-start.2) | async-done | bytes 2097184 | tf_op jit(solution)/shard_map/all_to_all | solution.py:30
  414.3 1.9 convert_reduce_fusion.1
  416.5 1.4 fusion.32
  417.9 87.4 %psum.14 = f32[]{:T(128)} all-reduce(f32[]{:T(128)} %get-tuple-element.186), channel_id=1, replica_groups=mesh['rep'=4,'dp'=32] {'rep','dp'}, use_global_device_ids=true, to_apply=%region_10.11 | all-reduce | flops 1 | bytes 8 | tf_op jit(solution)/shard_map/psum | solution.py:184
  506.7 79.2 %all-reduce.2.cloned.1.call-done = f32[768,128]{1,0:T(8,128)} async-done(((f32[768,128]{1,0:T(8,128)}), f32[768,128]{1,0:T(8,128)}) %all-reduce.2.cloned.1.call-update) | async-done | bytes 393232 | tf_op jit(solution)/shard_map/psum | solution.py:184
  586.0 1.8 copy.73
  (499 shorter events, 107.7 us)
Async XLA Ops:
  7.2 43.9 %copy-start = (bf16[768,128]{1,0:T(8,128)(2,1)S(1)}, bf16[768,128]{1,0:T(8,128)(2,1)}, u32[]{:S(2)}) copy-start(bf16[768,128]{1,0:T(8,128)(2,1)} %param.29) | copy-start | bytes 589828
  7.2 185.6 %all-gather.2.cloned.1.call-start = ((), (), s32[]{:S(2)}) async-start(), calls=%async_computation.3 | async-start | bytes 4325376 | tf_op jit(solution)/shard_map/all_gather | solution.py:18
  9.7 39.6 %copy-start.10 = (f32[768]{0:T(1024)S(1)}, f32[768]{0:T(1024)}, u32[]{:S(2)}) copy-start(f32[768]{0:T(1024)} %param.28) | copy-start | bytes 9220
  9.8 39.6 %copy-start.11 = (f32[768]{0:T(1024)S(1)}, f32[768]{0:T(1024)}, u32[]{:S(2)}) copy-start(f32[768]{0:T(1024)} %param.27) | copy-start | bytes 9220
  48.8 3.1 copy-start.13
  49.3 3.6 copy-start.9
  49.3 3.6 copy-start.14
  49.9 1.1 copy-start.4
  51.7 345.2 %copy-start.8 = (f32[976]{0:T(1024)}, f32[976]{0:T(1024)S(1)}, u32[]{:S(2)}) copy-start(f32[976]{0:T(1024)S(1)} %add_rsqrt_fusion) | copy-start | bytes 11716
  51.9 147.0 %copy-start.6 = (f32[976,128]{1,0:T(8,128)}, f32[976,128]{1,0:T(8,128)S(1)}, u32[]{:S(2)}) copy-start(f32[976,128]{1,0:T(8,128)S(1)} %broadcast_multiply_fusion) | copy-start | bytes 1499140
  198.9 45.7 %copy-start.12 = (s32[8]{0:T(128)S(1)}, s32[8]{0:T(128)}, u32[]{:S(2)}) copy-start(s32[8]{0:T(128)} %param.22) | copy-start | bytes 100
  231.2 13.4 %all-to-all-start = ((f32[32,8,4]{1,2,0:T(4,128)}), f32[32,8,4]{1,2,0:T(4,128)S(1)}, u32[]{:S(2)}, u32[]{:S(2)}) async-start(f32[32,8,4]{1,2,0:T(4,128)} %copy.39), calls=%async_computation | async-start | bytes 131072 | tf_op jit(solution)/shard_map/all_to_all | solution.py:155
  246.1 11.0 %all-to-all-start.1 = ((f32[8,32,4]{0,2,1:T(4,128)}), f32[8,32,4]{0,2,1:T(4,128)S(1)}, u32[]{:S(2)}, u32[]{:S(2)}) async-start(f32[8,32,4]{0,2,1:T(4,128)} %fusion.40), calls=%async_computation.1 | async-start | bytes 131072 | tf_op jit(solution)/shard_map/all_to_all | solution.py:157
  260.5 3.0 copy-start.1
  264.8 0.8 copy-start.2
  268.9 3.0 copy-start.1
  273.2 0.8 copy-start.2
  277.3 3.0 copy-start.1
  281.7 0.8 copy-start.2
  285.7 3.0 copy-start.1
  290.1 0.8 copy-start.2
  294.2 3.0 copy-start.1
  298.5 0.8 copy-start.2
  302.6 3.0 copy-start.1
  306.9 0.8 copy-start.2
  311.0 3.0 copy-start.1
  315.3 0.8 copy-start.2
  319.4 3.0 copy-start.1
  323.8 0.8 copy-start.2
  327.8 3.0 copy-start.1
  332.2 0.8 copy-start.2
  336.3 3.0 copy-start.1
  340.6 0.8 copy-start.2
  344.7 3.0 copy-start.1
  349.1 0.8 copy-start.2
  353.1 3.0 copy-start.1
  357.5 0.8 copy-start.2
  361.6 3.0 copy-start.1
  365.9 0.8 copy-start.2
  370.0 3.0 copy-start.1
  374.3 0.8 copy-start.2
  378.4 3.0 copy-start.1
  382.7 0.8 copy-start.2
  386.8 3.0 copy-start.1
  391.2 0.8 copy-start.2
  392.0 6.1 %copy-start.7 = (f32[976,128]{1,0:T(8,128)S(1)}, f32[976,128]{1,0:T(8,128)}, u32[]{:S(2)}) copy-start(f32[976,128]{1,0:T(8,128)} %copy-done.6) | copy-start | bytes 1499140
  392.0 24.5 %copy-start.5 = (bf16[976,768]{1,0:T(8,128)(2,1)S(1)}, bf16[976,768]{1,0:T(8,128)(2,1)}, u32[]{:S(2)}) copy-start(bf16[976,768]{1,0:T(8,128)(2,1)} %copy-done.4) | copy-start | bytes 4497412
  392.0 22.3 %all-to-all-start.2 = ((bf16[32,8,32,128]{3,2,1,0:T(8,128)(2,1)}), bf16[32,8,32,128]{3,2,1,0:T(8,128)(2,1)}, u32[]{:S(2)}, u32[]{:S(2)}) async-start(bf16[32,8,32,128]{3,2,1,0:T(8,128)(2,1)} %bitcast.97), calls=%async_computation.2 | async-start | bytes 4194304 | tf_op jit(solution)/shard_map/all_to_all | solution.py:30
  396.9 109.0 %copy-start.3 = (f32[4,180,128]{2,1,0:T(8,128)S(1)}, f32[4,180,128]{2,1,0:T(8,128)}, u32[]{:S(2)}) copy-start(f32[4,180,128]{2,1,0:T(8,128)} %get-tuple-element.153) | copy-start | bytes 1105924
  396.9 189.1 %all-reduce.2.cloned.1.call-start = ((), (), s32[]{:S(2)}) async-start(), calls=%async_computation.4 | async-start | bytes 786432 | tf_op jit(solution)/shard_map/psum | solution.py:184
  396.9 19.4 %slice-start = ((f32[976]{0:T(1024)}), f32[256]{0:T(256)S(1)}, s32[]{:S(2)}) async-start(f32[976]{0:T(1024)} %copy-done.8), calls=%async_computation.5 | async-start | bytes 2048 | tf_op jit(solution)/shard_map/slice | solution.py:176
Sparse Core Ops, SparseCore 0:
  53.0 139.7 all-gather.1
  418.0 167.9 all-reduce.1
where the time goes:
time: 598 us; the launch traced here: 596 us
  waiting for transfers between devices  249 us (42%)
  matrix products  120 us (20%)
  blocking collectives  87.4 us (15%)
  local copies, waits for them, and re-layouts  61.1 us (10%)
  other arithmetic  44.3 us (7%)
  between operations  16.1 us (3%)
  starting transfers between devices  15 us (3%)
    all_gather x1, waiting for transfers between devices, in_one_piece(): out = lax.all_gather(both, axis, axis=dim, tiled=True)  140 us
    psum x1, blocking collectives, per_device(): proj_total, loss_total = lax.psum((local_sum, loss_sum), ('rep', 'dp'))  87.4 us
    psum x1, waiting for transfers between devices, per_device(): proj_total, loss_total = lax.psum((local_sum, loss_sum), ('rep', 'dp'))  79.2 us
    dot_general x32, matrix products, token_scores(): lax.dot_general(query_flat, flat_block, (((1,), (1,)), ((), ())), preferr...  40.4 us
    dot_general x1, matrix products, encode_rows(): jnp.dot(activated, down_weight, preferred_element_type=jnp.float32)  39 us
    convert_element_type x16, other arithmetic, token_grads(): (weights * factor[:, :, None]).reshape(-1, item_count * pass_len)  27.2 us
    mul x32, local copies, waits for them, and re-layouts, token_grads(): weights * factor[:, :, None]  23 us
    dot_general x16, matrix products, token_grads(): lax.dot_general(sim_grad, query_flat, (((0,), (0,)), ((), ())), preferred...  21.4 us
  transfers between devices with their start and end apart: 5, of which 5 were waited for; matrix products, arithmetic and copies ran while one was open for 0% of the time, Pallas kernels for 0%

commit v1 on v0

--- a/solution.py
+++ b/solution.py
@@ -181,7 +181,7 @@
     local_sum = lax.dot_general(
         hidden, all_back, (((0,), (0,)), ((), ())), preferred_element_type=jnp.float32
     )
-    proj_total, loss_total = lax.psum((local_sum, loss_sum), ("rep", "dp"))
+    proj_total, loss_total = lax.psum(lax.psum((local_sum, loss_sum), "dp"), "rep")
     mean_loss = loss_total / (query_count * lax.axis_size("rep") * groups)
     return (mean_loss, passage_grad, proj_total)
 

time: 598 us -> 838 us (1.40)
  waiting for transfers between devices: 249 us -> 470 us
  blocking collectives: 87.4 us -> 107 us
    psum x1 -> x2, waiting for transfers between devices: 79.2 us -> 300 us  [the longest x1 300 us: per_device(): lax.psum((local_sum, loss_sum), 'dp')]
    psum x1 -> x2, blocking collectives: 87.4 us -> 107 us  [the longest x1 66.6 us: per_device(): lax.psum((local_sum, loss_sum), 'dp')]
  transfers between devices with their start and end apart: 5 -> 6, of which waited for: 5 -> 5; matrix products, arithmetic and copies ran while one was open for 0% -> 0% of each run, Pallas kernels for 0% -> 0%
where the time goes in v1:
time: 838 us; the launch traced here: 834 us
  waiting for transfers between devices  470 us (56%)
  matrix products  120 us (14%)
  blocking collectives  107 us (13%)
  local copies, waits for them, and re-layouts  61.1 us (7%)
  other arithmetic  42.9 us (5%)
  between operations  15.9 us (2%)
  starting transfers between devices  15.1 us (2%)
    psum x1, waiting for transfers between devices, per_device(): lax.psum((local_sum, loss_sum), 'dp')  300 us
    all_gather x1, waiting for transfers between devices, in_one_piece(): out = lax.all_gather(both, axis, axis=dim, tiled=True)  140 us
    psum x1, blocking collectives, per_device(): lax.psum((local_sum, loss_sum), 'dp')  66.6 us
    dot_general x32, matrix products, token_scores(): lax.dot_general(query_flat, flat_block, (((1,), (1,)), ((), ())), preferr...  40.4 us
    psum x1, blocking collectives, per_device(): lax.psum(lax.psum((local_sum, loss_sum), 'dp'), 'rep')  40.1 us
    dot_general x1, matrix products, encode_rows(): jnp.dot(activated, down_weight, preferred_element_type=jnp.float32)  39 us
    convert_element_type x16, other arithmetic, token_grads(): (weights * factor[:, :, None]).reshape(-1, item_count * pass_len)  25.8 us
    mul x32, local copies, waits for them, and re-layouts, token_grads(): weights * factor[:, :, None]  23 us
  transfers between devices with their start and end apart: 6, of which 5 were waited for; matrix products, arithmetic and copies ran while one was open for 0% of the time, Pallas kernels for 0%

profile of v1, /device:TPU:1, one launch (start us, length us, event | category | flops | bytes accessed | tf_op | source)
XLA Modules:
  0.0 834.4 jit_solution(11840823748585069281)
XLA Ops:
  7.2 1.4 copy.36
  9.8 39.0 %fusion.79 = (f32[976]{0:T(1024)S(1)}, f32[976,768]{1,0:T(8,128)S(1)}) fusion(f32[768]{0:T(1024)} %param.26, bf16[3072,768]{1,0:T(8,128)(2,1)} %param.25, f32[3072]{0:T(1024)} %param.24, bf16[768,3072]{1,0:T(8,128)(2,1)} %param.23, bf16[720,768]{1,0:T(8,128)(2,1)} %reshape.220, bf16[256,768]{1,0:T(8,128)(2,1)} %bitcast.103), kind=kOutput, calls=%fused_computation.118 | convolution fusion | flops 9416821760 | bytes 13953856 | tf_op jit(solution)/shard_map/dot_general | solution.py:41
  53.0 139.8 %all-gather.2.cloned.1.call-done = bf16[256,32,129]{2,1,0:T(8,128)(2,1)} async-done(((bf16[8,32,129]{2,1,0:T(8,128)(2,1)}), bf16[256,32,129]{2,1,0:T(8,128)(2,1)}) %all-gather.2.cloned.1.call-update) | async-done | bytes 2113552 | tf_op jit(solution)/shard_map/all_gather | solution.py:18
  192.7 2.7 convert_reduce_fusion
  195.6 3.3 split.8
  198.9 31.5 %while.23 = (s32[]{:T(128)}, f32[16,16,4]{1,0,2:T(8,128)S(1)}, bf16[16,512,128]{2,1,0:T(8,128)(2,1)}, bf16[720,128]{1,0:T(8,128)(2,1)S(1)}, bf16[4,180]{1,0:T(4,...) while((s32[]{:T(128)}, f32[16,16,4]{1,0,2:T(8,128)S(1)}, bf16[16,512,128]{2,1,0:T(8,128)(2,1)}, ...), condition=%wide.region_6.7_spmd, body=%wide.region_3.6_spmd.sunk | while | flops 95480976 | bytes 6281597 | solution.py:154
  198.9 1.3 multiply_exponential_fusion.4
  200.8 1.3 multiply_exponential_fusion.4
  202.8 1.3 multiply_exponential_fusion.4
  204.8 1.3 multiply_exponential_fusion.4
  206.8 1.3 multiply_exponential_fusion.4
  208.7 1.3 multiply_exponential_fusion.4
  210.7 1.3 multiply_exponential_fusion.4
  212.7 1.3 multiply_exponential_fusion.4
  214.6 1.3 multiply_exponential_fusion.4
  218.6 1.3 multiply_exponential_fusion.4
  220.5 1.3 multiply_exponential_fusion.4
  224.5 1.3 multiply_exponential_fusion.4
  226.5 1.3 multiply_exponential_fusion.4
  231.1 6.2 all-to-all-start
  237.4 7.2 all-to-all-done
  246.0 3.9 all-to-all-start.1
  249.9 7.2 all-to-all-done.1
  257.1 133.4 %while.24 = (s32[]{:T(128)}, f32[4,180,128]{2,1,0:T(8,128)}, bf16[16,512,128]{2,1,0:T(8,128)(2,1)}, bf16[16,512,128]{2,1,0:T(8,128)(2,1)}, bf16[720,128]{1,0:T(8...) while((s32[]{:T(128)}, f32[4,180,128]{2,1,0:T(8,128)}, ...), condition=%wide.region_14.15_spmd.clone, body=%wide.region_12.14_spmd.clone.sunk | while | flops 285514432 | bytes 21625324 | solution.py:169
  260.5 1.6 multiply_convert_fusion.3
  263.3 1.3 convolution_add_fusion.2
  268.8 1.6 multiply_convert_fusion.3
  271.7 1.3 convolution_add_fusion.2
  277.2 1.6 multiply_convert_fusion.3
  280.0 1.3 convolution_add_fusion.2
  285.5 1.6 multiply_convert_fusion.3
  288.4 1.3 convolution_add_fusion.2
  293.8 1.6 multiply_convert_fusion.3
  296.7 1.3 convolution_add_fusion.2
  302.2 1.6 multiply_convert_fusion.3
  305.0 1.3 convolution_add_fusion.2
  310.5 1.6 multiply_convert_fusion.3
  313.3 1.3 convolution_add_fusion.2
  318.8 1.6 multiply_convert_fusion.3
  321.7 1.3 convolution_add_fusion.2
  327.2 1.6 multiply_convert_fusion.3
  330.0 1.3 convolution_add_fusion.2
  335.5 1.6 multiply_convert_fusion.3
  338.4 1.3 convolution_add_fusion.2
  343.9 1.6 multiply_convert_fusion.3
  346.7 1.3 convolution_add_fusion.2
  352.2 1.6 multiply_convert_fusion.3
  355.0 1.3 convolution_add_fusion.2
  360.5 1.6 multiply_convert_fusion.3
  363.4 1.3 convolution_add_fusion.2
  368.9 1.6 multiply_convert_fusion.3
  371.7 1.3 convolution_add_fusion.2
  377.2 1.6 multiply_convert_fusion.3
  380.0 1.3 convolution_add_fusion.2
  385.5 1.6 multiply_convert_fusion.3
  388.4 1.3 convolution_add_fusion.2
  390.5 4.9 all-to-all-start.2
  397.0 15.8 %all-to-all-done.2 = bf16[32,8,32,128]{3,2,1,0:T(8,128)(2,1)} async-done(((bf16[32,8,32,128]{3,2,1,0:T(8,128)(2,1)}), bf16[32,8,32,128]{3,2,1,0:T(8,128)(2,1)}, u32[]{:S(2)}, u32[]{:S(2)}) %all-to-all-start.2) | async-done | bytes 2097184 | tf_op jit(solution)/shard_map/all_to_all | solution.py:30
  412.8 1.9 convert_reduce_fusion.1
  415.0 1.4 fusion.32
  416.5 300.3 %all-reduce.3.cloned.1.call-done = f32[768,128]{1,0:T(8,128)} async-done(((f32[768,128]{1,0:T(8,128)}), f32[768,128]{1,0:T(8,128)}) %all-reduce.3.cloned.1.call-update) | async-done | bytes 393232 | tf_op jit(solution)/shard_map/psum | solution.py:184
  716.8 66.6 %psum.28 = f32[]{:T(128)} all-reduce(f32[]{:T(128)} %get-tuple-element.186), channel_id=1, replica_groups=mesh['rep'=4,'dp'=32] {'dp'}, use_global_device_ids=true, to_apply=%region_10.11 | all-reduce | flops 1 | bytes 8 | tf_op jit(solution)/shard_map/psum | solution.py:184
  783.4 40.1 %psum.29 = f32[]{:T(128)} all-reduce(f32[]{:T(128)} %psum.28), channel_id=1, replica_groups=mesh['rep'=4,'dp'=32] {'rep'}, use_global_device_ids=true, to_apply=%region_11.12 | all-reduce | flops 1 | bytes 8 | tf_op jit(solution)/shard_map/psum | solution.py:184
  825.0 1.8 copy.74
  (503 shorter events, 109.1 us)
Async XLA Ops:
  7.2 43.8 %copy-start = (bf16[768,128]{1,0:T(8,128)(2,1)S(1)}, bf16[768,128]{1,0:T(8,128)(2,1)}, u32[]{:S(2)}) copy-start(bf16[768,128]{1,0:T(8,128)(2,1)} %param.29) | copy-start | bytes 589828
  7.2 185.5 %all-gather.2.cloned.1.call-start = ((), (), s32[]{:S(2)}) async-start(), calls=%async_computation.3 | async-start | bytes 4325376 | tf_op jit(solution)/shard_map/all_gather | solution.py:18
  9.7 39.6 %copy-start.10 = (f32[768]{0:T(1024)S(1)}, f32[768]{0:T(1024)}, u32[]{:S(2)}) copy-start(f32[768]{0:T(1024)} %param.28) | copy-start | bytes 9220
  9.8 39.6 %copy-start.11 = (f32[768]{0:T(1024)S(1)}, f32[768]{0:T(1024)}, u32[]{:S(2)}) copy-start(f32[768]{0:T(1024)} %param.27) | copy-start | bytes 9220
  48.8 3.1 copy-start.13
  49.3 3.6 copy-start.9
  49.3 3.6 copy-start.14
  49.9 1.1 copy-start.4
  51.7 343.8 %copy-start.8 = (f32[976]{0:T(1024)}, f32[976]{0:T(1024)S(1)}, u32[]{:S(2)}) copy-start(f32[976]{0:T(1024)S(1)} %add_rsqrt_fusion) | copy-start | bytes 11716
  51.9 147.0 %copy-start.6 = (f32[976,128]{1,0:T(8,128)}, f32[976,128]{1,0:T(8,128)S(1)}, u32[]{:S(2)}) copy-start(f32[976,128]{1,0:T(8,128)S(1)} %broadcast_multiply_fusion) | copy-start | bytes 1499140
  198.9 45.7 %copy-start.12 = (s32[8]{0:T(128)S(1)}, s32[8]{0:T(128)}, u32[]{:S(2)}) copy-start(s32[8]{0:T(128)} %param.22) | copy-start | bytes 100
  231.1 13.4 %all-to-all-start = ((f32[32,8,4]{1,2,0:T(4,128)}), f32[32,8,4]{1,2,0:T(4,128)S(1)}, u32[]{:S(2)}, u32[]{:S(2)}) async-start(f32[32,8,4]{1,2,0:T(4,128)} %copy.39), calls=%async_computation | async-start | bytes 131072 | tf_op jit(solution)/shard_map/all_to_all | solution.py:155
  246.0 11.0 %all-to-all-start.1 = ((f32[8,32,4]{0,2,1:T(4,128)}), f32[8,32,4]{0,2,1:T(4,128)S(1)}, u32[]{:S(2)}, u32[]{:S(2)}) async-start(f32[8,32,4]{0,2,1:T(4,128)} %fusion.40), calls=%async_computation.1 | async-start | bytes 131072 | tf_op jit(solution)/shard_map/all_to_all | solution.py:157
  260.4 2.9 copy-start.1
  264.7 0.8 copy-start.2
  268.7 2.9 copy-start.1
  273.0 0.8 copy-start.2
  277.1 2.9 copy-start.1
  281.4 0.8 copy-start.2
  285.4 2.9 copy-start.1
  289.7 0.8 copy-start.2
  293.8 2.9 copy-start.1
  298.0 0.8 copy-start.2
  302.1 2.9 copy-start.1
  306.3 0.8 copy-start.2
  310.4 2.9 copy-start.1
  314.7 0.8 copy-start.2
  318.7 2.9 copy-start.1
  323.0 0.8 copy-start.2
  327.1 2.9 copy-start.1
  331.4 0.8 copy-start.2
  335.4 2.9 copy-start.1
  339.7 0.8 copy-start.2
  343.8 2.9 copy-start.1
  348.0 0.8 copy-start.2
  352.1 2.9 copy-start.1
  356.4 0.8 copy-start.2
  360.4 2.9 copy-start.1
  364.7 0.8 copy-start.2
  368.8 2.9 copy-start.1
  373.0 0.8 copy-start.2
  377.1 2.9 copy-start.1
  381.4 0.8 copy-start.2
  385.4 2.9 copy-start.1
  389.7 0.8 copy-start.2
  390.5 6.1 copy-start.7
  390.5 24.5 %copy-start.5 = (bf16[976,768]{1,0:T(8,128)(2,1)S(1)}, bf16[976,768]{1,0:T(8,128)(2,1)}, u32[]{:S(2)}) copy-start(bf16[976,768]{1,0:T(8,128)(2,1)} %copy-done.4) | copy-start | bytes 4497412
  390.5 22.3 %all-to-all-start.2 = ((bf16[32,8,32,128]{3,2,1,0:T(8,128)(2,1)}), bf16[32,8,32,128]{3,2,1,0:T(8,128)(2,1)}, u32[]{:S(2)}, u32[]{:S(2)}) async-start(bf16[32,8,32,128]{3,2,1,0:T(8,128)(2,1)} %bitcast.97), calls=%async_computation.2 | async-start | bytes 4194304 | tf_op jit(solution)/shard_map/all_to_all | solution.py:30
  395.4 428.7 %copy-start.3 = (f32[4,180,128]{2,1,0:T(8,128)S(1)}, f32[4,180,128]{2,1,0:T(8,128)}, u32[]{:S(2)}) copy-start(f32[4,180,128]{2,1,0:T(8,128)} %get-tuple-element.153) | copy-start | bytes 1105924
  395.4 321.3 %all-reduce.3.cloned.1.call-start = ((), (), s32[]{:S(2)}) async-start(), calls=%async_computation.4 | async-start | bytes 786432 | tf_op jit(solution)/shard_map/psum | solution.py:184
  395.5 19.4 %slice-start = ((f32[976]{0:T(1024)}), f32[256]{0:T(256)S(1)}, s32[]{:S(2)}) async-start(f32[976]{0:T(1024)} %copy-done.8), calls=%async_computation.6 | async-start | bytes 2048 | tf_op jit(solution)/shard_map/slice | solution.py:176
  416.4 408.6 %all-reduce.5.cloned.1.call-start = ((), (), s32[]{:S(2)}) async-start(), calls=%async_computation.5 | async-start | bytes 786432 | tf_op jit(solution)/shard_map/psum | solution.py:184
Sparse Core Ops, SparseCore 0:
  53.0 139.7 all-gather.1
  416.5 300.1 all-reduce.2
  719.3 61.3 all-reduce.4
